TPU v7x, 32 devices: a whole 2x2x4 slice. The times are simulated.
32 devices in a mesh: band: 32 (over z, y, x, core).
Axes of the slice: x: 2, y: 2, z: 4, core: 2. Of those that a mesh axis runs over, the one named last changes fastest.
Arguments:
- jones_start: float32 [32, 32, 512], P('band'), may hold values from -1.5 to 1.5
- visible: bfloat16 [32, 8, 4096], P('band'), may hold values from -6 to 6
- coherent: bfloat16 [32, 32, 4096], P('band'), may hold values from -1 to 1
- stations: int32 [2, 4096], replicated, may hold values from 0 to 511, as said below
- weights: float32 [32, 512], P('band'), may hold values from 0.2 to 2
- multiplier_start: float32 [32, 32, 512], P('band'), may hold values from -2 to 2
Outputs:
- jones_final: float32 [32, 32, 512], P('band')
- multiplier_final: float32 [32, 32, 512], P('band')
- coefficients: float32 [96, 512], P(None, 'band')
Inputs may be any that keep to these rules, and one draw needn't show every extreme that they name: Rows 0 and 1 of each column name two different stations; the same baselines serve every subband.
All inputs are finite; a program needn't handle non-finite values.
Results may differ from a plain program's by a relative error of at most 0.0003.
Values sent between devices are 32-bit elements; how exact they have to be, the bound alone decides.
A program may use at most 64 MiB of HBM per device.

v0:
```python
import jax
import jax.numpy as jnp
from jax import lax
from jax.sharding import PartitionSpec as P

ITERS = 2
PENALTY = 1.0
STEP_SIZE = 0.05
PAIR_LIST = ((0, 0), (0, 1), (0, 2), (1, 1), (1, 2), (2, 2))


def matrix_product(first_real, first_imag, second_real, second_imag):

    def contract(lhs_part, rhs_part):
        return jnp.sum(lhs_part[:, :, :, None, :] * rhs_part[:, None, :, :, :], axis=2)

    real_part = contract(first_real, second_real) - contract(first_imag, second_imag)
    imag_part = contract(first_real, second_imag) + contract(first_imag, second_real)
    return (real_part, imag_part)


def band_loss(
    jones_band, visible_band, coherent_band, stations, target_band, multiplier_band, weight_band
):
    baseline_count = stations.shape[1]
    direction_count = jones_band.shape[0] // 8
    station_first = jnp.take(jones_band, stations[0], axis=1).reshape(
        direction_count, 2, 2, 2, baseline_count
    )
    station_second = jnp.take(jones_band, stations[1], axis=1).reshape(
        direction_count, 2, 2, 2, baseline_count
    )
    sky_model = coherent_band.astype(jnp.float32).reshape(direction_count, 2, 2, 2, baseline_count)
    inner_real, inner_imag = matrix_product(
        station_first[:, 0], station_first[:, 1], sky_model[:, 0], sky_model[:, 1]
    )
    herm_real = jnp.swapaxes(station_second[:, 0], 1, 2)
    herm_imag = -jnp.swapaxes(station_second[:, 1], 1, 2)
    model_real, model_imag = matrix_product(inner_real, inner_imag, herm_real, herm_imag)
    predicted = jnp.stack([jnp.sum(model_real, axis=0), jnp.sum(model_imag, axis=0)])
    misfit = visible_band.astype(jnp.float32).reshape(2, 2, 2, baseline_count) - predicted
    data_scale = jones_band.shape[1] / (2.0 * baseline_count)
    distance = jones_band - target_band
    return (
        data_scale * jnp.sum(misfit * misfit)
        + jnp.sum(multiplier_band * distance)
        + 0.5 * PENALTY * jnp.sum(weight_band[None, :] * distance * distance)
    )


def descend(
    jones_band, visible_band, coherent_band, stations, target_band, multiplier_band, weight_band
):
    slope_fn = jax.grad(band_loss)
    slope = slope_fn(
        jones_band, visible_band, coherent_band, stations, target_band, multiplier_band, weight_band
    )
    jones_band = jones_band - STEP_SIZE * slope
    return jones_band


def solve_normal(normal_matrix, right_side):
    gram_aa, gram_ab, gram_ac, gram_bb, gram_bc, gram_cc = [
        normal_matrix[position] for position in range(6)
    ]
    cofac_aa = gram_bb * gram_cc - gram_bc * gram_bc
    cofac_ab = gram_ac * gram_bc - gram_ab * gram_cc
    cofac_ac = gram_ab * gram_bc - gram_ac * gram_bb
    cofac_bb = gram_aa * gram_cc - gram_ac * gram_ac
    cofac_bc = gram_ab * gram_ac - gram_aa * gram_bc
    cofac_cc = gram_aa * gram_bb - gram_ab * gram_ab
    determinant = gram_aa * cofac_aa + gram_ab * cofac_ab + gram_ac * cofac_ac
    inverse_det = 1.0 / determinant
    first_term = right_side[0]
    second_term = right_side[1]
    third_term = right_side[2]
    coeff_a = (cofac_aa * first_term + cofac_ab * second_term + cofac_ac * third_term) * inverse_det
    coeff_b = (cofac_ab * first_term + cofac_bb * second_term + cofac_bc * third_term) * inverse_det
    coeff_c = (cofac_ac * first_term + cofac_bc * second_term + cofac_cc * third_term) * inverse_det
    return jnp.stack([coeff_a, coeff_b, coeff_c])


def local(jones_start, visible, coherent, stations, weights, multiplier_start):
    band_count = lax.axis_size("band")
    band_index = lax.axis_index("band")
    abscissa = -1.0 + 2.0 * band_index.astype(jnp.float32) / (band_count - 1)
    basis_local = (jnp.ones((), jnp.float32), abscissa, 1.5 * abscissa * abscissa - 0.5)
    weight_band = weights[0]
    visible_band = visible[0]
    coherent_band = coherent[0]
    station_share = weights.shape[1] // band_count
    products = jnp.stack(
        [basis_local[first_idx] * basis_local[second_idx] for first_idx, second_idx in PAIR_LIST]
    )
    normal_term = PENALTY * products[:, None] * weight_band[None, :]
    normal_solver = lax.psum(normal_term, "band")

    def iteration(turn_index, carried):
        jones_band, multiplier_band, owned_prior = carried
        combined = multiplier_band + PENALTY * weight_band[None, :] * jones_band
        weighted_terms = jnp.stack([basis_local[term_index] * combined for term_index in range(3)])
        full_sums = lax.psum(weighted_terms, "band")
        coefficients = solve_normal(normal_solver, full_sums)
        owned_coeff = lax.dynamic_slice_in_dim(
            coefficients, band_index * station_share, station_share, 2
        )
        target_band = (
            basis_local[0] * coefficients[0]
            + basis_local[1] * coefficients[1]
            + basis_local[2] * coefficients[2]
        )
        multiplier_band = multiplier_band + PENALTY * weight_band[None, :] * (
            jones_band - target_band
        )
        jones_band = descend(
            jones_band,
            visible_band,
            coherent_band,
            stations,
            target_band,
            multiplier_band,
            weight_band,
        )
        return (jones_band, multiplier_band, owned_coeff)

    owned_start = jnp.zeros((3, jones_start.shape[1], station_share), jnp.float32)
    jones_band, multiplier_band, owned_coeff = lax.fori_loop(
        0, ITERS, iteration, (jones_start[0], multiplier_start[0], owned_start)
    )
    coeff_rows = owned_coeff.reshape(
        owned_coeff.shape[0] * owned_coeff.shape[1], owned_coeff.shape[2]
    )
    return (jones_band[None], multiplier_band[None], coeff_rows)


def solution(mesh):
    return jax.shard_map(
        local,
        mesh=mesh,
        in_specs=(
            P("band", None, None),
            P("band", None, None),
            P("band", None, None),
            P(),
            P("band", None),
            P("band", None, None),
        ),
        out_specs=(P("band", None, None), P("band", None, None), P(None, "band")),
        check_vma=False,
    )
```

profile of v0, /device:TPU:8, one launch (start us, length us, event | category | flops | bytes accessed | tf_op | source)
XLA Modules:
  0.0 373.0 jit_solution(7236217893154198396)
XLA Ops:
  7.2 0.8 copy.133
  8.0 0.8 copy.134
  8.9 0.8 broadcast_multiply_fusion.1
  9.7 40.5 %psum.17 = f32[6,512]{1,0:T(8,128)S(1)} all-reduce(f32[6,512]{1,0:T(8,128)S(1)} %broadcast_multiply_fusion.1), channel_id=1, replica_groups=mesh['band'=32] {'band'}, use_global_device_ids=true, to_apply=%region_0.0 | all-reduce | flops 3072 | bytes 24576 | tf_op jit(solution)/shard_map/psum | solution.py:96
  50.1 0.6 multiply_add_fusion.2
  50.8 313.9 %while.17 = (s32[]{:T(128)}, f32[32,512]{1,0:T(8,128)S(1)}, f32[32,512]{1,0:T(8,128)S(1)}, f32[3,32,16]{2,1,0:T(8,128)}, f32[1,512]{1,0:T(1,128)}, /*index=5*/f3...) while((s32[]{:T(128)}, f32[32,512]{1,0:T(8,128)S(1)}, ...), condition=%wide.region_27.0_spmd, body=%wide.region_1.28_spmd.sunk | while | flops 6967298 | bytes 52347996 | solution.py:127
  50.8 0.7 multiply_bitcast_fusion.4
  51.5 0.7 pad_maximum_fusion.2
  52.3 0.9 fusion.32
  53.2 0.6 compare_select_fusion.3
  53.8 14.1 %gather_fusion.1 = f32[4096,32]{1,0:T(8,128)} fusion(f32[32,512]{0,1:T(8,128)S(1)} %copy.101, s32[4096]{0:T(1024)S(1)} %get-tuple-element.581), kind=kCustom, calls=%fused_computation.1.clone.clone.1 | custom fusion | bytes 1064960 | tf_op jit(solution)/shard_map/while/body/eval_jaxpr/jvp(jit(_take))/gather | solution.py:27
  67.9 3.6 select_bitcast_fusion.5
  72.5 0.9 copy.106
  73.4 0.9 copy.108
  75.0 14.1 %gather_fusion = f32[4096,32]{1,0:T(8,128)} fusion(f32[32,512]{0,1:T(8,128)S(1)} %copy.101, s32[4096]{0:T(1024)S(1)} %get-tuple-element.578), kind=kCustom, calls=%fused_computation.clone.clone.1 | custom fusion | bytes 1064960 | tf_op jit(solution)/shard_map/while/body/eval_jaxpr/jvp(jit(_take))/gather | solution.py:30
  89.1 3.6 select_bitcast_fusion.4
  94.4 0.6 multiply_reduce_fusion.24
  95.2 0.6 multiply_reduce_fusion.25
  96.4 1.3 multiply_reduce_fusion.26
  97.9 0.6 multiply_reduce_fusion.27
  100.1 2.0 copy.114
  102.9 0.6 copy.112
  103.5 22.7 %scatter_custom_fusion.8 = f32[32,512]{0,1:T(8,128)S(1)} fusion(s32[4096]{0:T(1024)} %get-tuple-element.603, f32[4096,32]{1,0:T(8,128)} %copy.114, f32[]{:T(128)} %constant.70.clone.25..sunk), kind=kCustom, calls=%fused_computation.50.clone.1 | custom fusion | flops 131072 | bytes 66048 | tf_op jit(solution)/shard_map/while/body/eval_jaxpr/transpose(jvp(jit(_take)))/scatter-add | solution.py:27
  126.2 57.3 %all-reduce.6.cloned.1.call-done = f32[3,32,512]{2,1,0:T(8,128)} async-done(((f32[3,32,512]{2,1,0:T(8,128)}), f32[3,32,512]{2,1,0:T(8,128)}) %all-reduce.6.cloned.1.call-update) | async-done | bytes 196624 | tf_op jit(solution)/shard_map/while/body/eval_jaxpr/psum | solution.py:102
  183.5 1.0 add_add_fusion.2
  184.7 22.5 %scatter_fusion = f32[32,512]{0,1:T(8,128)S(1)} fusion(f32[32,512]{0,1:T(8,128)S(1)} %copy.102, s32[4096]{0:T(1024)S(1)} %get-tuple-element.577, f32[4096,32]{1,0:T(8,128)S(1)} %copy.112), kind=kCustom, calls=%fused_computation.2.clone.1 | custom fusion | flops 131072 | bytes 1589248 | tf_op jit(solution)/shard_map/while/body/eval_jaxpr/transpose(jvp(jit(_take)))/scatter-add | solution.py:30
  207.4 0.7 fusion.36
  208.1 0.7 multiply_bitcast_fusion.4
  208.8 0.7 pad_maximum_fusion.2
  209.6 0.9 fusion.32
  210.5 0.6 compare_select_fusion.3
  211.2 14.1 %gather_fusion.1 = f32[4096,32]{1,0:T(8,128)} fusion(f32[32,512]{0,1:T(8,128)S(1)} %copy.101, s32[4096]{0:T(1024)S(1)} %get-tuple-element.581), kind=kCustom, calls=%fused_computation.1.clone.clone.1 | custom fusion | bytes 1064960 | tf_op jit(solution)/shard_map/while/body/eval_jaxpr/jvp(jit(_take))/gather | solution.py:27
  225.3 3.6 select_bitcast_fusion.5
  229.8 0.9 copy.106
  230.7 0.9 copy.108
  232.3 14.1 %gather_fusion = f32[4096,32]{1,0:T(8,128)} fusion(f32[32,512]{0,1:T(8,128)S(1)} %copy.101, s32[4096]{0:T(1024)S(1)} %get-tuple-element.578), kind=kCustom, calls=%fused_computation.clone.clone.1 | custom fusion | bytes 1064960 | tf_op jit(solution)/shard_map/while/body/eval_jaxpr/jvp(jit(_take))/gather | solution.py:30
  246.4 3.6 select_bitcast_fusion.4
  251.7 0.6 multiply_reduce_fusion.24
  252.5 0.6 multiply_reduce_fusion.25
  253.8 1.3 multiply_reduce_fusion.26
  255.2 0.6 multiply_reduce_fusion.27
  257.4 2.0 copy.114
  260.8 22.7 %scatter_custom_fusion.8 = f32[32,512]{0,1:T(8,128)S(1)} fusion(s32[4096]{0:T(1024)} %get-tuple-element.603, f32[4096,32]{1,0:T(8,128)} %copy.114, f32[]{:T(128)} %constant.70.clone.25..sunk), kind=kCustom, calls=%fused_computation.50.clone.1 | custom fusion | flops 131072 | bytes 66048 | tf_op jit(solution)/shard_map/while/body/eval_jaxpr/transpose(jvp(jit(_take)))/scatter-add | solution.py:27
  283.5 56.6 %all-reduce.6.cloned.1.call-done = f32[3,32,512]{2,1,0:T(8,128)} async-done(((f32[3,32,512]{2,1,0:T(8,128)}), f32[3,32,512]{2,1,0:T(8,128)}) %all-reduce.6.cloned.1.call-update) | async-done | bytes 196624 | tf_op jit(solution)/shard_map/while/body/eval_jaxpr/psum | solution.py:102
  340.1 1.0 add_add_fusion.2
  341.3 22.5 %scatter_fusion = f32[32,512]{0,1:T(8,128)S(1)} fusion(f32[32,512]{0,1:T(8,128)S(1)} %copy.102, s32[4096]{0:T(1024)S(1)} %get-tuple-element.577, f32[4096,32]{1,0:T(8,128)S(1)} %copy.112), kind=kCustom, calls=%fused_computation.2.clone.1 | custom fusion | flops 131072 | bytes 1589248 | tf_op jit(solution)/shard_map/while/body/eval_jaxpr/transpose(jvp(jit(_take)))/scatter-add | solution.py:30
  364.0 0.7 fusion.36
  364.7 1.5 copy.85
  (147 shorter events, 14.5 us)
Async XLA Ops:
  50.8 132.8 %all-reduce.6.cloned.1.call-start = ((), (), s32[]{:S(2)}) async-start(), calls=%async_computation | async-start | bytes 393216 | tf_op jit(solution)/shard_map/while/body/eval_jaxpr/psum | solution.py:102
  72.1 2.1 copy-start.5
  93.3 0.8 copy-start.6
  93.3 1.0 copy-start
  93.3 1.1 copy-start.1
  95.1 1.3 copy-start.7
  98.6 0.7 copy-start.14
  102.4 81.1 %copy-start.8 = (f32[1,512]{1,0:T(1,128)S(1)}, f32[1,512]{1,0:T(1,128)}, u32[]{:S(2)}) copy-start(f32[1,512]{1,0:T(1,128)} %get-tuple-element.667) | copy-start | bytes 6148 | tf_op jit(solution)/shard_map/while
  102.4 81.1 %copy-start.9 = (f32[1,512]{1,0:T(1,128)S(1)}, f32[1,512]{1,0:T(1,128)}, u32[]{:S(2)}) copy-start(f32[1,512]{1,0:T(1,128)} %get-tuple-element.666) | copy-start | bytes 6148 | tf_op jit(solution)/shard_map/while
  102.4 81.1 %copy-start.10 = (f32[1,512]{1,0:T(1,128)S(1)}, f32[1,512]{1,0:T(1,128)}, u32[]{:S(2)}) copy-start(f32[1,512]{1,0:T(1,128)} %get-tuple-element.663) | copy-start | bytes 6148 | tf_op jit(solution)/shard_map/while
  102.5 81.1 %copy-start.11 = (f32[1,512]{1,0:T(1,128)S(1)}, f32[1,512]{1,0:T(1,128)}, u32[]{:S(2)}) copy-start(f32[1,512]{1,0:T(1,128)} %get-tuple-element.671) | copy-start | bytes 6148 | tf_op jit(solution)/shard_map/while
  102.5 81.1 %copy-start.12 = (f32[1,512]{1,0:T(1,128)S(1)}, f32[1,512]{1,0:T(1,128)}, u32[]{:S(2)}) copy-start(f32[1,512]{1,0:T(1,128)} %get-tuple-element.670) | copy-start | bytes 6148 | tf_op jit(solution)/shard_map/while
  102.5 81.1 %copy-start.13 = (f32[1,512]{1,0:T(1,128)S(1)}, f32[1,512]{1,0:T(1,128)}, u32[]{:S(2)}) copy-start(f32[1,512]{1,0:T(1,128)} %get-tuple-element.669) | copy-start | bytes 6148 | tf_op jit(solution)/shard_map/while
  184.7 22.7 %copy-start.2 = (f32[3,32,512]{2,1,0:T(8,128)S(1)}, f32[3,32,512]{2,1,0:T(8,128)}, u32[]{:S(2)}) copy-start(f32[3,32,512]{2,1,0:T(8,128)} %all-reduce.6.cloned.1.call-done) | copy-start | bytes 589828 | tf_op jit(solution)/shard_map/while
  208.1 132.0 %all-reduce.6.cloned.1.call-start = ((), (), s32[]{:S(2)}) async-start(), calls=%async_computation | async-start | bytes 393216 | tf_op jit(solution)/shard_map/while/body/eval_jaxpr/psum | solution.py:102
  229.4 2.1 copy-start.5
  250.6 0.8 copy-start.6
  250.6 1.0 copy-start
  250.6 1.1 copy-start.1
  252.5 1.3 copy-start.7
  255.9 0.7 copy-start.14
  259.8 80.3 %copy-start.8 = (f32[1,512]{1,0:T(1,128)S(1)}, f32[1,512]{1,0:T(1,128)}, u32[]{:S(2)}) copy-start(f32[1,512]{1,0:T(1,128)} %get-tuple-element.667) | copy-start | bytes 6148 | tf_op jit(solution)/shard_map/while
  259.8 80.3 %copy-start.9 = (f32[1,512]{1,0:T(1,128)S(1)}, f32[1,512]{1,0:T(1,128)}, u32[]{:S(2)}) copy-start(f32[1,512]{1,0:T(1,128)} %get-tuple-element.666) | copy-start | bytes 6148 | tf_op jit(solution)/shard_map/while
  259.8 80.3 %copy-start.10 = (f32[1,512]{1,0:T(1,128)S(1)}, f32[1,512]{1,0:T(1,128)}, u32[]{:S(2)}) copy-start(f32[1,512]{1,0:T(1,128)} %get-tuple-element.663) | copy-start | bytes 6148 | tf_op jit(solution)/shard_map/while
  259.8 80.3 %copy-start.11 = (f32[1,512]{1,0:T(1,128)S(1)}, f32[1,512]{1,0:T(1,128)}, u32[]{:S(2)}) copy-start(f32[1,512]{1,0:T(1,128)} %get-tuple-element.671) | copy-start | bytes 6148 | tf_op jit(solution)/shard_map/while
  259.8 80.3 %copy-start.12 = (f32[1,512]{1,0:T(1,128)S(1)}, f32[1,512]{1,0:T(1,128)}, u32[]{:S(2)}) copy-start(f32[1,512]{1,0:T(1,128)} %get-tuple-element.670) | copy-start | bytes 6148 | tf_op jit(solution)/shard_map/while
  259.8 80.3 %copy-start.13 = (f32[1,512]{1,0:T(1,128)S(1)}, f32[1,512]{1,0:T(1,128)}, u32[]{:S(2)}) copy-start(f32[1,512]{1,0:T(1,128)} %get-tuple-element.669) | copy-start | bytes 6148 | tf_op jit(solution)/shard_map/while
  341.3 22.7 %copy-start.2 = (f32[3,32,512]{2,1,0:T(8,128)S(1)}, f32[3,32,512]{2,1,0:T(8,128)}, u32[]{:S(2)}) copy-start(f32[3,32,512]{2,1,0:T(8,128)} %all-reduce.6.cloned.1.call-done) | copy-start | bytes 589828 | tf_op jit(solution)/shard_map/while
  364.7 1.5 copy-start.3
  364.7 1.5 copy-start.4
Sparse Core Ops, SparseCore 0:
  57.1 126.3 all-reduce.5
  214.4 125.6 all-reduce.5
where the time goes:
time: 374 us; the launch traced here: 373 us
  other arithmetic  123 us (33%)
  waiting for transfers between devices  114 us (30%)
  local copies, waits for them, and re-layouts  80.8 us (22%)
  blocking collectives  40.5 us (11%)
  between operations  14 us (4%)
    psum x2, waiting for transfers between devices, iteration(): full_sums = lax.psum(weighted_terms, 'band')  114 us
    scatter-add x2, other arithmetic, band_loss(): jnp.take(jones_band, stations[0], axis=1)  45.4 us
    scatter-add x2, other arithmetic, band_loss(): jnp.take(jones_band, stations[1], axis=1)  45 us
    psum x1, blocking collectives, local(): normal_solver = lax.psum(normal_term, 'band')  40.5 us
    gather x2, local copies, waits for them, and re-layouts, band_loss(): jnp.take(jones_band, stations[0], axis=1)  28.2 us
    gather x2, local copies, waits for them, and re-layouts, band_loss(): jnp.take(jones_band, stations[1], axis=1)  28.2 us
    select_n x4, other arithmetic, band_loss(): jnp.take(jones_band, stations[0], axis=1)  8.44 us
  transfers between devices with their start and end apart: 2, of which 2 were waited for; matrix products, arithmetic and copies ran while one was open for 39% of the time, Pallas kernels for 0%

commit v1 on v0

--- a/solution.py
+++ b/solution.py
@@ -99,7 +99,8 @@
         jones_band, multiplier_band, owned_prior = carried
         combined = multiplier_band + PENALTY * weight_band[None, :] * jones_band
         weighted_terms = jnp.stack([basis_local[term_index] * combined for term_index in range(3)])
-        full_sums = lax.psum(weighted_terms, "band")
+        parts = lax.all_gather(weighted_terms, "band")
+        full_sums = jnp.sum(parts, axis=0)
         coefficients = solve_normal(normal_solver, full_sums)
         owned_coeff = lax.dynamic_slice_in_dim(
             coefficients, band_index * station_share, station_share, 2

time: 374 us -> 272 us (0.73)
  waiting for transfers between devices: 114 us -> 0.07 us
  other arithmetic: 123 us -> 129 us
    psum x2 -> x0, waiting for transfers between devices: 114 us -> none  [iteration(): full_sums = lax.psum(weighted_terms, 'band')]
    reduce_sum x0 -> x2, other arithmetic: none -> 6.8 us  [iteration(): full_sums = jnp.sum(parts, axis=0)]
  transfers between devices with their start and end apart: 2 -> 2, of which waited for: 2 -> 0; matrix products, arithmetic and copies ran while one was open for 39% -> 56% of each run, Pallas kernels for 0% -> 0%
where the time goes in v1:
time: 272 us; the launch traced here: 269 us
  other arithmetic  129 us (47%)
  local copies, waits for them, and re-layouts  84.3 us (31%)
  blocking collectives  40.5 us (15%)
  between operations  14 us (5%)
    scatter-add x2, other arithmetic, band_loss(): jnp.take(jones_band, stations[0], axis=1)  45.4 us
    scatter-add x2, other arithmetic, band_loss(): jnp.take(jones_band, stations[1], axis=1)  45 us
    psum x1, blocking collectives, local(): normal_solver = lax.psum(normal_term, 'band')  40.5 us
    gather x2, local copies, waits for them, and re-layouts, band_loss(): jnp.take(jones_band, stations[0], axis=1)  28.2 us
    gather x2, local copies, waits for them, and re-layouts, band_loss(): jnp.take(jones_band, stations[1], axis=1)  28.1 us
    select_n x4, other arithmetic, band_loss(): jnp.take(jones_band, stations[0], axis=1)  8.43 us
    select_n x2, other arithmetic, band_loss(): jnp.take(jones_band, stations[1], axis=1)  7.23 us
    reduce_sum x2, other arithmetic, iteration(): full_sums = jnp.sum(parts, axis=0)  6.8 us
  transfers between devices with their start and end apart: 2, of which 0 were waited for; matrix products, arithmetic and copies ran while one was open for 56% of the time, Pallas kernels for 0%

profile of v1, /device:TPU:8, one launch (start us, length us, event | category | flops | bytes accessed | tf_op | source)
XLA Modules:
  0.0 269.1 jit_solution(15739374982398202927)
XLA Ops:
  7.2 0.8 copy.158
  8.0 0.8 copy.157
  8.9 0.8 broadcast_multiply_fusion.1
  9.7 40.5 %psum.7 = f32[6,512]{1,0:T(8,128)S(1)} all-reduce(f32[6,512]{1,0:T(8,128)S(1)} %broadcast_multiply_fusion.1), channel_id=1, replica_groups=mesh['band'=32] {'band'}, use_global_device_ids=true, to_apply=%region_0.0 | all-reduce | flops 3072 | bytes 24576 | tf_op jit(solution)/shard_map/psum | solution.py:96
  50.1 0.6 multiply_add_fusion.2
  50.8 210.0 %while.17 = (s32[]{:T(128)}, f32[32,512]{1,0:T(8,128)S(1)}, f32[32,512]{1,0:T(8,128)S(1)}, f32[3,32,16]{2,1,0:T(8,128)}, f32[1,512]{1,0:T(1,128)}, /*index=5*/f3...) while((s32[]{:T(128)}, f32[32,512]{1,0:T(8,128)S(1)}, ...), condition=%wide.region_27.0_spmd, body=%wide.region_1.28_spmd.sunk | while | flops 8441858 | bytes 75875416 | solution.py:128
  50.8 0.7 multiply_bitcast_fusion.4
  51.5 0.7 pad_maximum_fusion.2
  52.2 0.9 fusion.32
  53.1 0.6 compare_select_fusion.3
  53.8 1.3 reshape.304
  55.2 14.1 %gather_fusion.1 = f32[4096,32]{1,0:T(8,128)} fusion(f32[32,512]{0,1:T(8,128)S(1)} %copy.126, s32[4096]{0:T(1024)S(1)} %get-tuple-element.581), kind=kCustom, calls=%fused_computation.1.clone.clone.1 | custom fusion | bytes 1064960 | tf_op jit(solution)/shard_map/while/body/eval_jaxpr/jvp(jit(_take))/gather | solution.py:27
  69.3 3.6 %select_bitcast_fusion.5 = f32[32,4096]{0,1:T(8,128)S(1)} fusion(f32[4096,32]{1,0:T(8,128)} %gather_fusion.1, pred[4096]{0:T(1024)(128)(4,1)S(1)} %compare_and_fusion.5), kind=kLoop, calls=%fused_computation.4.clone.1 | loop fusion | flops 131072 | bytes 1052672 | tf_op jit(solution)/shard_map/while/body/eval_jaxpr/jvp(jit(_take))/select_n | solution.py:27
  74.3 0.7 reshape.301
  75.4 0.9 copy.131
  76.3 0.9 copy.133
  77.8 14.1 %gather_fusion = f32[4096,32]{1,0:T(8,128)} fusion(f32[32,512]{0,1:T(8,128)S(1)} %copy.126, s32[4096]{0:T(1024)S(1)} %get-tuple-element.578), kind=kCustom, calls=%fused_computation.clone.clone.1 | custom fusion | bytes 1064960 | tf_op jit(solution)/shard_map/while/body/eval_jaxpr/jvp(jit(_take))/gather | solution.py:30
  91.8 3.6 %select_bitcast_fusion.4 = f32[32,4096]{0,1:T(8,128)S(1)} fusion(f32[4096,32]{1,0:T(8,128)} %gather_fusion, pred[4096]{0:T(1024)(128)(4,1)S(1)} %compare_and_fusion.4), kind=kLoop, calls=%fused_computation.5.clone.1 | loop fusion | flops 131072 | bytes 1052672 | tf_op jit(solution)/shard_map/while/body/eval_jaxpr/jvp(jit(_take))/select_n | solution.py:30
  97.1 0.6 multiply_reduce_fusion.24
  97.9 0.6 multiply_reduce_fusion.25
  99.2 1.3 multiply_reduce_fusion.26
  101.6 0.6 multiply_reduce_fusion.27
  103.2 2.0 copy.139
  105.8 22.7 %scatter_custom_fusion.8 = f32[32,512]{0,1:T(8,128)S(1)} fusion(s32[4096]{0:T(1024)} %get-tuple-element.603, f32[4096,32]{1,0:T(8,128)} %copy.139, f32[]{:T(128)} %constant.68.clone.25..sunk), kind=kCustom, calls=%fused_computation.50.clone.1 | custom fusion | flops 131072 | bytes 66048 | tf_op jit(solution)/shard_map/while/body/eval_jaxpr/transpose(jvp(jit(_take)))/scatter-add | solution.py:27
  128.6 3.4 %reduce_sum.357 = f32[3,32,512]{2,1,0:T(8,128)S(1)} reduce(f32[32,3,32,512]{3,2,1,0:T(8,128)} %bitcast.199, f32[]{:T(128)} %constant.68.clone.25..sunk), dimensions={0}, to_apply=%region_2.0 | reduce | flops 1523712 | bytes 6488068 | tf_op jit(solution)/shard_map/while/body/eval_jaxpr/reduce_sum | solution.py:103
  132.4 22.5 %scatter_fusion = f32[32,512]{0,1:T(8,128)S(1)} fusion(f32[32,512]{0,1:T(8,128)S(1)} %copy.127, s32[4096]{0:T(1024)S(1)} %copy-done.5, f32[4096,32]{1,0:T(8,128)S(1)} %copy.137), kind=kCustom, calls=%fused_computation.2.clone.1 | custom fusion | flops 131072 | bytes 1589248 | tf_op jit(solution)/shard_map/while/body/eval_jaxpr/transpose(jvp(jit(_take)))/scatter-add | solution.py:30
  155.0 0.7 fusion.36
  155.8 0.7 multiply_bitcast_fusion.4
  156.5 0.7 pad_maximum_fusion.2
  157.2 0.9 fusion.32
  158.8 1.3 reshape.304
  160.2 14.1 %gather_fusion.1 = f32[4096,32]{1,0:T(8,128)} fusion(f32[32,512]{0,1:T(8,128)S(1)} %copy.126, s32[4096]{0:T(1024)S(1)} %get-tuple-element.581), kind=kCustom, calls=%fused_computation.1.clone.clone.1 | custom fusion | bytes 1064960 | tf_op jit(solution)/shard_map/while/body/eval_jaxpr/jvp(jit(_take))/gather | solution.py:27
  174.2 3.6 %select_bitcast_fusion.5 = f32[32,4096]{0,1:T(8,128)S(1)} fusion(f32[4096,32]{1,0:T(8,128)} %gather_fusion.1, pred[4096]{0:T(1024)(128)(4,1)S(1)} %compare_and_fusion.5), kind=kLoop, calls=%fused_computation.4.clone.1 | loop fusion | flops 131072 | bytes 1052672 | tf_op jit(solution)/shard_map/while/body/eval_jaxpr/jvp(jit(_take))/select_n | solution.py:27
  179.3 0.7 reshape.301
  180.4 0.9 copy.131
  181.2 0.9 copy.133
  182.7 14.1 %gather_fusion = f32[4096,32]{1,0:T(8,128)} fusion(f32[32,512]{0,1:T(8,128)S(1)} %copy.126, s32[4096]{0:T(1024)S(1)} %get-tuple-element.578), kind=kCustom, calls=%fused_computation.clone.clone.1 | custom fusion | bytes 1064960 | tf_op jit(solution)/shard_map/while/body/eval_jaxpr/jvp(jit(_take))/gather | solution.py:30
  196.8 3.6 %select_bitcast_fusion.4 = f32[32,4096]{0,1:T(8,128)S(1)} fusion(f32[4096,32]{1,0:T(8,128)} %gather_fusion, pred[4096]{0:T(1024)(128)(4,1)S(1)} %compare_and_fusion.4), kind=kLoop, calls=%fused_computation.5.clone.1 | loop fusion | flops 131072 | bytes 1052672 | tf_op jit(solution)/shard_map/while/body/eval_jaxpr/jvp(jit(_take))/select_n | solution.py:30
  202.0 0.6 multiply_reduce_fusion.24
  202.9 0.6 multiply_reduce_fusion.25
  204.1 1.3 multiply_reduce_fusion.26
  206.6 0.6 multiply_reduce_fusion.27
  208.2 2.0 copy.139
  210.7 22.7 %scatter_custom_fusion.8 = f32[32,512]{0,1:T(8,128)S(1)} fusion(s32[4096]{0:T(1024)} %get-tuple-element.603, f32[4096,32]{1,0:T(8,128)} %copy.139, f32[]{:T(128)} %constant.68.clone.25..sunk), kind=kCustom, calls=%fused_computation.50.clone.1 | custom fusion | flops 131072 | bytes 66048 | tf_op jit(solution)/shard_map/while/body/eval_jaxpr/transpose(jvp(jit(_take)))/scatter-add | solution.py:27
  233.6 3.4 %reduce_sum.357 = f32[3,32,512]{2,1,0:T(8,128)S(1)} reduce(f32[32,3,32,512]{3,2,1,0:T(8,128)} %bitcast.199, f32[]{:T(128)} %constant.68.clone.25..sunk), dimensions={0}, to_apply=%region_2.0 | reduce | flops 1523712 | bytes 6488068 | tf_op jit(solution)/shard_map/while/body/eval_jaxpr/reduce_sum | solution.py:103
  237.4 22.5 %scatter_fusion = f32[32,512]{0,1:T(8,128)S(1)} fusion(f32[32,512]{0,1:T(8,128)S(1)} %copy.127, s32[4096]{0:T(1024)S(1)} %copy-done.5, f32[4096,32]{1,0:T(8,128)S(1)} %copy.137), kind=kCustom, calls=%fused_computation.2.clone.1 | custom fusion | flops 131072 | bytes 1589248 | tf_op jit(solution)/shard_map/while/body/eval_jaxpr/transpose(jvp(jit(_take)))/scatter-add | solution.py:30
  260.0 0.7 fusion.36
  260.7 1.5 copy.110
  (149 shorter events, 16.7 us)
Async XLA Ops:
  50.8 77.8 %all-gather.5.cloned.1.call-start = ((), (), s32[]{:S(2)}) async-start(), calls=%async_computation | async-start | bytes 6488064 | tf_op jit(solution)/shard_map/while/body/eval_jaxpr/all_gather | solution.py:102
  73.5 0.8 copy-start.6
  96.0 1.0 copy-start
  96.0 1.0 copy-start.1
  97.8 1.2 copy-start.3
  105.2 23.3 %copy-start.7 = (f32[1,512]{1,0:T(1,128)S(1)}, f32[1,512]{1,0:T(1,128)}, u32[]{:S(2)}) copy-start(f32[1,512]{1,0:T(1,128)} %get-tuple-element.662) | copy-start | bytes 6148 | tf_op jit(solution)/shard_map/while
  105.2 23.4 %copy-start.14 = (f32[1,512]{1,0:T(1,128)S(1)}, f32[1,512]{1,0:T(1,128)}, u32[]{:S(2)}) copy-start(f32[1,512]{1,0:T(1,128)} %get-tuple-element.668) | copy-start | bytes 6148 | tf_op jit(solution)/shard_map/while
  128.6 3.5 %copy-start.8 = (f32[1,512]{1,0:T(1,128)S(1)}, f32[1,512]{1,0:T(1,128)}, u32[]{:S(2)}) copy-start(f32[1,512]{1,0:T(1,128)} %get-tuple-element.667) | copy-start | bytes 6148 | tf_op jit(solution)/shard_map/while
  128.6 3.5 %copy-start.9 = (f32[1,512]{1,0:T(1,128)S(1)}, f32[1,512]{1,0:T(1,128)}, u32[]{:S(2)}) copy-start(f32[1,512]{1,0:T(1,128)} %get-tuple-element.666) | copy-start | bytes 6148 | tf_op jit(solution)/shard_map/while
  128.6 3.5 %copy-start.10 = (f32[1,512]{1,0:T(1,128)S(1)}, f32[1,512]{1,0:T(1,128)}, u32[]{:S(2)}) copy-start(f32[1,512]{1,0:T(1,128)} %get-tuple-element.663) | copy-start | bytes 6148 | tf_op jit(solution)/shard_map/while
  128.6 3.5 %copy-start.11 = (f32[1,512]{1,0:T(1,128)S(1)}, f32[1,512]{1,0:T(1,128)}, u32[]{:S(2)}) copy-start(f32[1,512]{1,0:T(1,128)} %get-tuple-element.671) | copy-start | bytes 6148 | tf_op jit(solution)/shard_map/while
  128.6 3.5 %copy-start.12 = (f32[1,512]{1,0:T(1,128)S(1)}, f32[1,512]{1,0:T(1,128)}, u32[]{:S(2)}) copy-start(f32[1,512]{1,0:T(1,128)} %get-tuple-element.670) | copy-start | bytes 6148 | tf_op jit(solution)/shard_map/while
  128.6 3.5 %copy-start.13 = (f32[1,512]{1,0:T(1,128)S(1)}, f32[1,512]{1,0:T(1,128)}, u32[]{:S(2)}) copy-start(f32[1,512]{1,0:T(1,128)} %get-tuple-element.669) | copy-start | bytes 6148 | tf_op jit(solution)/shard_map/while
  128.6 3.8 %copy-start.5 = (s32[4096]{0:T(1024)S(1)}, s32[4096]{0:T(1024)}, u32[]{:S(2)}) copy-start(s32[4096]{0:T(1024)} %get-tuple-element.577) | copy-start | bytes 49156 | tf_op jit(solution)/shard_map/while
  155.7 77.8 %all-gather.5.cloned.1.call-start = ((), (), s32[]{:S(2)}) async-start(), calls=%async_computation | async-start | bytes 6488064 | tf_op jit(solution)/shard_map/while/body/eval_jaxpr/all_gather | solution.py:102
  178.4 0.8 copy-start.6
  201.0 1.0 copy-start
  201.0 1.0 copy-start.1
  202.8 1.2 copy-start.3
  210.1 23.3 %copy-start.7 = (f32[1,512]{1,0:T(1,128)S(1)}, f32[1,512]{1,0:T(1,128)}, u32[]{:S(2)}) copy-start(f32[1,512]{1,0:T(1,128)} %get-tuple-element.662) | copy-start | bytes 6148 | tf_op jit(solution)/shard_map/while
  210.1 23.4 %copy-start.14 = (f32[1,512]{1,0:T(1,128)S(1)}, f32[1,512]{1,0:T(1,128)}, u32[]{:S(2)}) copy-start(f32[1,512]{1,0:T(1,128)} %get-tuple-element.668) | copy-start | bytes 6148 | tf_op jit(solution)/shard_map/while
  233.5 3.5 %copy-start.8 = (f32[1,512]{1,0:T(1,128)S(1)}, f32[1,512]{1,0:T(1,128)}, u32[]{:S(2)}) copy-start(f32[1,512]{1,0:T(1,128)} %get-tuple-element.667) | copy-start | bytes 6148 | tf_op jit(solution)/shard_map/while
  233.6 3.5 %copy-start.9 = (f32[1,512]{1,0:T(1,128)S(1)}, f32[1,512]{1,0:T(1,128)}, u32[]{:S(2)}) copy-start(f32[1,512]{1,0:T(1,128)} %get-tuple-element.666) | copy-start | bytes 6148 | tf_op jit(solution)/shard_map/while
  233.6 3.5 %copy-start.10 = (f32[1,512]{1,0:T(1,128)S(1)}, f32[1,512]{1,0:T(1,128)}, u32[]{:S(2)}) copy-start(f32[1,512]{1,0:T(1,128)} %get-tuple-element.663) | copy-start | bytes 6148 | tf_op jit(solution)/shard_map/while
  233.6 3.5 %copy-start.11 = (f32[1,512]{1,0:T(1,128)S(1)}, f32[1,512]{1,0:T(1,128)}, u32[]{:S(2)}) copy-start(f32[1,512]{1,0:T(1,128)} %get-tuple-element.671) | copy-start | bytes 6148 | tf_op jit(solution)/shard_map/while
  233.6 3.5 %copy-start.12 = (f32[1,512]{1,0:T(1,128)S(1)}, f32[1,512]{1,0:T(1,128)}, u32[]{:S(2)}) copy-start(f32[1,512]{1,0:T(1,128)} %get-tuple-element.670) | copy-start | bytes 6148 | tf_op jit(solution)/shard_map/while
  233.6 3.5 %copy-start.13 = (f32[1,512]{1,0:T(1,128)S(1)}, f32[1,512]{1,0:T(1,128)}, u32[]{:S(2)}) copy-start(f32[1,512]{1,0:T(1,128)} %get-tuple-element.669) | copy-start | bytes 6148 | tf_op jit(solution)/shard_map/while
  233.6 3.8 %copy-start.5 = (s32[4096]{0:T(1024)S(1)}, s32[4096]{0:T(1024)}, u32[]{:S(2)}) copy-start(s32[4096]{0:T(1024)} %get-tuple-element.577) | copy-start | bytes 49156 | tf_op jit(solution)/shard_map/while
  260.7 1.5 copy-start.2
  260.7 1.5 copy-start.4
Sparse Core Ops, SparseCore 0:
  54.4 69.0 all-gather.4
  159.4 69.0 all-gather.4
